TPU v7x, 32 devices: a whole 2x2x4 slice. The times are simulated.
32 devices in a mesh: fsdp: 4 (over y, x), tenant: 4 (over z), dp: 2 (over core).
Axes of the slice: x: 2, y: 2, z: 4, core: 2. Of those that a mesh axis runs over, the one named last changes fastest.
Arguments:
- tokens: bfloat16 [3072, 5120], P(('fsdp', 'dp'), 'tenant'), may hold values from -6 to 6
- block_tenant_index: int32 [48], P(('fsdp', 'dp')), may hold values from 0 to 7
- ranks: int32 [8], replicated, may hold values from 16 to 64, as said below
- frozen_up_weight: bfloat16 [5120, 14336], P(('fsdp', 'dp'), 'tenant'), may hold values from -0.078125 to 0.078125
- tenant_down_adapters: bfloat16 [8, 64, 5120], P('tenant'), may hold values from -0.078125 to 0.078125
- tenant_up_adapters: bfloat16 [8, 64, 14336], P('tenant'), may hold values from -0.75 to 0.75
- cotangent: bfloat16 [3072, 14336], P(('fsdp', 'dp'), 'tenant'), may hold values from -6 to 6
Outputs:
- hidden_out: bfloat16 [3072, 14336], P(('fsdp', 'dp'), 'tenant')
- grad_tokens: bfloat16 [3072, 5120], P(('fsdp', 'dp'), 'tenant')
- grad_down: float32 [8, 64, 5120], P('dp', None, 'tenant')
- grad_up: float32 [8, 64, 14336], P('dp', None, 'tenant')
Inputs may be any that keep to these rules, and one draw needn't show every extreme that they name: `ranks`: multiples of 16; some tenant has rank 64.
All inputs are finite; a program needn't handle non-finite values.
Results may differ from a plain program's by a relative error of at most 0.0034.
Values may be sent and summed in bfloat16 or wider, within the bound.
No kernel may reach another device: no remote copies, remote signals or barrier semaphores. Data moves between devices by JAX's collectives and lax.ppermute only.
A program may use at most 128 MiB of HBM per device.

v0:
```python
import jax
import jax.numpy as jnp
from jax import lax
from jax.sharding import PartitionSpec as P

BLOCK = 64
alpha_scale = 32.0


def make_gain(block_tenant_index, ranks, rows, largest_rank):
    tenants = ranks.shape[0]
    rows_tenant = jnp.repeat(block_tenant_index, BLOCK, total_repeat_length=rows)
    columns = jnp.arange(tenants * largest_rank, dtype=jnp.int32)
    col_tenant = columns // largest_rank
    col_slot = columns % largest_rank
    ranks_col = jnp.repeat(ranks, largest_rank, total_repeat_length=tenants * largest_rank)
    keep = (rows_tenant[:, None] == col_tenant[None, :]) & (col_slot[None, :] < ranks_col[None, :])
    scale_col = alpha_scale / ranks_col.astype(jnp.float32)
    return jnp.where(keep, scale_col[None, :], jnp.float32(0.0))


def shards(
    tokens,
    block_tenant_index,
    ranks,
    frozen_up_weight,
    tenant_down_adapters,
    tenant_up_adapters,
    cotangent,
):
    rows = tokens.shape[0]
    local_d = tokens.shape[1]
    local_f = cotangent.shape[1]
    tenants = ranks.shape[0]
    largest_rank = tenant_down_adapters.shape[1]
    gain = make_gain(block_tenant_index, ranks, rows, largest_rank)
    whole = lax.all_gather(tokens, "tenant", axis=1, tiled=True)
    weight = lax.all_gather(frozen_up_weight, ("fsdp", "dp"), axis=0, tiled=True)
    down_part, up_adapter_slice = (
        lax.all_to_all(tenant_down_adapters, "tenant", split_axis=2, concat_axis=0, tiled=True),
        lax.all_to_all(tenant_up_adapters, "tenant", split_axis=2, concat_axis=0, tiled=True),
    )
    local_down = down_part.reshape(tenants * largest_rank, local_d)
    partial_proj = lax.dot_general(
        tokens, local_down, (((1,), (1,)), ((), ())), preferred_element_type=jnp.float32
    )
    proj = lax.psum(partial_proj, "tenant")
    flattened_up = up_adapter_slice.reshape(tenants * largest_rank, local_f)
    adapted = (proj * gain).astype(jnp.bfloat16)
    base = jnp.dot(whole, weight, preferred_element_type=jnp.float32)
    hidden_out = (base + jnp.dot(adapted, flattened_up, preferred_element_type=jnp.float32)).astype(
        jnp.bfloat16
    )
    back_part = lax.dot_general(
        cotangent, flattened_up, (((1,), (1,)), ((), ())), preferred_element_type=jnp.float32
    )
    back = lax.psum(back_part, "tenant")
    adapted_grad = (back * gain).astype(jnp.bfloat16)
    base_back = lax.dot_general(
        cotangent, weight, (((1,), (1,)), ((), ())), preferred_element_type=jnp.float32
    )
    grad_base = lax.psum_scatter(base_back, "tenant", scatter_dimension=1, tiled=True)
    grad_tokens = (
        grad_base + jnp.dot(adapted_grad, local_down, preferred_element_type=jnp.float32)
    ).astype(jnp.bfloat16)
    up_term = lax.dot_general(
        adapted, cotangent, (((0,), (0,)), ((), ())), preferred_element_type=jnp.float32
    )
    down_term = lax.dot_general(
        adapted_grad, tokens, (((0,), (0,)), ((), ())), preferred_element_type=jnp.float32
    )
    up_term = up_term.reshape(tenants, largest_rank, local_f)
    down_term = down_term.reshape(tenants, largest_rank, local_d)
    down_share, up_share = (
        lax.psum_scatter(down_term, "dp", scatter_dimension=0, tiled=True),
        lax.psum_scatter(up_term, "dp", scatter_dimension=0, tiled=True),
    )
    grad_down, grad_up = lax.psum((down_share, up_share), "fsdp")
    return (hidden_out, grad_tokens, grad_down, grad_up)


def solution(mesh):
    return jax.shard_map(
        shards,
        mesh=mesh,
        in_specs=(
            P(("fsdp", "dp"), "tenant"),
            P(("fsdp", "dp")),
            P(),
            P(("fsdp", "dp"), "tenant"),
            P("tenant", None, None),
            P("tenant", None, None),
            P(("fsdp", "dp"), "tenant"),
        ),
        out_specs=(
            P(("fsdp", "dp"), "tenant"),
            P(("fsdp", "dp"), "tenant"),
            P("dp", None, "tenant"),
            P("dp", None, "tenant"),
        ),
        check_vma=False,
    )
```

profile of v0, /device:TPU:0, one launch (start us, length us, event | category | flops | bytes accessed | tf_op | source)
XLA Modules:
  0.0 692.7 jit_solution(15375952981959615952)
XLA Ops:
  8.0 0.0 copy-start
  8.0 6.4 copy.13
  14.5 4.7 reshape.322
  19.1 6.3 all-to-all-start
  25.5 15.8 %copy.16 = bf16[2,64,14336]{1,0,2:T(2,128)(2,1)} copy(bf16[2,64,14336]{2,1,0:T(8,128)(2,1)} %param.16) | data formatting | bytes 7340032 | tf_op args[5]
  41.3 8.6 %reshape.320 = bf16[4,2,229376]{2,1,0:T(2,128)(2,1)} reshape(bf16[14336,2,64]{2,1,0:T(2,128)(2,1)} %bitcast.77) | data formatting | bytes 7340032
  49.9 7.1 %all-to-all-done = bf16[4,2,81920]{2,1,0:T(2,128)(2,1)} async-done(((bf16[4,2,81920]{2,1,0:T(2,128)(2,1)}), bf16[4,2,81920]{2,1,0:T(2,128)(2,1)}, u32[]{:S(2)}, u32[]{:S(2)}) %all-to-all-start) | async-done | bytes 1310752 | tf_op jit(solution)/shard_map/all_to_all | solution.py:40
  56.9 4.8 all-to-all-start.1
  61.8 0.0 all-reduce.5.cloned.1.call-start
  61.8 4.6 reshape.323
  66.4 7.4 %copy.19 = bf16[2,64,4,1280]{3,2,1,0:T(4,128)(2,1)} copy(bf16[2,64,4,1280]{1,0,3,2:T(2,128)(2,1)} %bitcast.82) | data formatting | bytes 2621440 | tf_op jit(solution)/shard_map/all_to_all | solution.py:40
  73.8 1.4 copy.15
  75.3 0.0 copy-start.3
  75.3 1.0 copy-done.3
  76.3 2.8 fusion.26
  79.1 64.2 %all-to-all-done.1 = bf16[4,2,229376]{2,1,0:T(2,128)(2,1)} async-done(((bf16[4,2,229376]{2,1,0:T(2,128)(2,1)}), bf16[4,2,229376]{2,1,0:T(2,128)(2,1)}, u32[]{:S(2)}, u32[]{:S(2)}) %all-to-all-start.1) | async-done | bytes 3670048 | tf_op jit(solution)/shard_map/all_to_all | solution.py:41
  143.3 8.4 %reshape.321 = bf16[14336,2,64]{2,1,0:T(2,128)(2,1)} reshape(bf16[4,2,229376]{2,1,0:T(2,128)(2,1)} %all-to-all-done.1) | data formatting | bytes 7340032
  151.7 18.7 %copy.20 = bf16[2,64,4,3584]{3,2,1,0:T(4,128)(2,1)} copy(bf16[2,64,4,3584]{1,0,3,2:T(2,128)(2,1)} %bitcast.76) | data formatting | bytes 7340032 | tf_op jit(solution)/shard_map/all_to_all | solution.py:41
  170.4 2.7 copy.18
  173.1 0.0 copy-start.2
  173.1 1.8 copy-done.2
  174.9 0.0 copy-done
  174.9 2.5 fusion.28
  177.4 0.0 all-reduce.5.cloned.1.call-update
  177.5 0.0 all-gather.5.cloned.1.call-start
  177.5 0.5 all-gather.5.cloned.1.call-update
  178.0 0.0 reduce-scatter.6.cloned.1.call-start
  178.1 0.0 copy-done.8
  178.1 0.7 fusion.23
  178.8 0.0 copy-done.7
  178.8 0.7 fusion.24
  179.5 0.0 copy-done.10
  179.5 0.1 add_add_fusion.1
  179.6 0.1 fusion.8
  179.7 3.8 fusion.16
  183.5 4.5 compare_select_fusion.2
  188.0 0.8 fusion.12
  188.8 0.1 and_select_fusion
  188.9 56.8 %all-reduce.5.cloned.1.call-done = (f32[384,512]{1,0:T(8,128)}, f32[384,512]{1,0:T(8,128)}) async-done(((f32[384,512]{1,0:T(8,128)}, f32[384,512]{1,0:T(8,128)}), (f32[384,512]{1,0:T(8,128)}, f32[384,512]{1,0:T(8,128)})) %all-reduce.5.cloned.1.call-update) | async-done | bytes 1572880 | tf_op jit(solution)/shard_map/psum | solution.py:47
  245.7 4.0 fusion.17
  249.7 0.0 reduce-scatter.6.cloned.1.call-update
  249.7 0.0 reduce-scatter.8.cloned.1.call-start
  249.8 7.1 %fusion.20 = f32[512,3584]{1,0:T(8,128)} fusion(bf16[384,3584]{1,0:T(8,128)(2,1)S(1)} %copy-done, f32[384,512]{1,0:T(8,128)S(1)} %copy-done.5, f32[512]{0:T(512)S(1)} %convert_divide_fusion, s32[512]{0:T(512)S(1)} %add_select_fusion, s32[384]{0:T(512)S(1)} %and_select_fusion, pred[512]{0:T(512)(128)(4,1)S(1)} %get-tuple-element.32), kind=kOutput, calls=%fused_computation.52 | convolution fusion | flops 1410269184 | bytes 10885120 | tf_op jit(solution)/shard_map/dot_general | solution.py:66
  256.9 0.0 reduce-scatter.8.cloned.1.call-update
  256.9 0.0 all-gather.3.cloned.1.call-start
  256.9 0.5 all-gather.3.cloned.1.call-update
  257.5 0.2 reduce-scatter.4.cloned.1.call-start
  257.7 96.2 %all-gather.5.cloned.1.call-done = bf16[5120,3584]{1,0:T(8,128)(2,1)} async-done(((bf16[640,3584]{1,0:T(8,128)(2,1)}), bf16[5120,3584]{1,0:T(8,128)(2,1)}) %all-gather.5.cloned.1.call-update) | async-done | bytes 36700176 | tf_op jit(solution)/shard_map/all_gather | solution.py:38
  353.9 22.1 %fusion.27 = f32[384,5120]{1,0:T(8,128)} fusion(bf16[384,3584]{1,0:T(8,128)(2,1)S(1)} %copy-done, bf16[5120,3584]{1,0:T(8,128)(2,1)} %all-gather.5.cloned.1.call-done), kind=kOutput, calls=%fused_computation.57 | convolution fusion | flops 14092861440 | bytes 47316992 | tf_op jit(solution)/shard_map/dot_general | solution.py:59
  376.0 0.0 reduce-scatter.4.cloned.1.call-update
  376.0 0.0 all-reduce.7.cloned.1.call-start
  376.1 0.0 reduce-scatter.6.cloned.1.call-done
  376.1 0.0 reduce-scatter.8.cloned.1.call-done
  376.1 0.5 all-reduce.7.cloned.1.call-update
  376.6 139.9 %all-gather.3.cloned.1.call-done = bf16[384,5120]{1,0:T(8,128)(2,1)} async-done(((bf16[384,1280]{1,0:T(8,128)(2,1)}), bf16[384,5120]{1,0:T(8,128)(2,1)}) %all-gather.3.cloned.1.call-update) | async-done | bytes 3932176 | tf_op jit(solution)/shard_map/all_gather | solution.py:37
  516.5 23.5 %fusion.25 = f32[384,3584]{1,0:T(8,128)} fusion(bf16[384,5120]{1,0:T(8,128)(2,1)} %all-gather.3.cloned.1.call-done, bf16[5120,3584]{1,0:T(8,128)(2,1)} %all-gather.5.cloned.1.call-done), kind=kOutput, calls=%fused_computation.55 | convolution fusion | flops 14092861440 | bytes 46137344 | tf_op jit(solution)/shard_map/dot_general | solution.py:50
  540.0 7.0 %fusion = bf16[384,3584]{1,0:T(8,128)(2,1)} fusion(f32[384,3584]{1,0:T(8,128)} %fusion.25, bf16[512,3584]{1,0:T(8,128)(2,1)} %bitcast.79, f32[384,512]{1,0:T(8,128)S(1)} %copy-done.5, f32[512]{0:T(512)S(1)} %convert_divide_fusion, s32[512]{0:T(512)S(1)} %add_select_fusion, s32[384]{0:T(512)S(1)} %and_select_fusion, pred[512]{0:T(512)(128)(4,1)S(1)} %get-tuple-element.32), kind=kOutput, calls=%fused_computation.1 | convolution fusion | flops 1413021696 | bytes 12720128 | tf_op jit(solution)/shard_map/dot_general | solution.py:51
  547.0 10.7 %reduce-scatter.4.cloned.1.call-done = f32[384,1280]{1,0:T(8,128)} async-done(((f32[384,5120]{1,0:T(8,128)}), f32[384,1280]{1,0:T(8,128)}) %reduce-scatter.4.cloned.1.call-update) | async-done | bytes 1966096 | tf_op jit(solution)/shard_map/reduce_scatter | solution.py:62
  557.7 0.0 copy-done.4
  557.7 3.3 fusion.1
  561.0 117.8 %all-reduce.7.cloned.1.call-done = (f32[4,64,1280]{2,1,0:T(8,128)}, f32[4,64,3584]{2,1,0:T(8,128)}) async-done(((f32[4,64,1280]{2,1,0:T(8,128)}, f32[4,64,3584]{2,1,0:T(8,128)}), (f32[4,64,1280]{2,1,0:T(8,128)}, f32[4,64,3584]{2,1,0:T(8,128)})) %all-reduce.7.cloned.1.call-update) | async-done | bytes 4980752 | tf_op jit(solution)/shard_map/psum | solution.py:78
  678.8 2.6 copy.29
  681.4 4.1 copy.30
  685.6 0.0 copy-done.1
  (16 shorter events, 0.1 us)
Async XLA Ops:
  8.0 166.9 %copy-start = (bf16[384,3584]{1,0:T(8,128)(2,1)S(1)}, bf16[384,3584]{1,0:T(8,128)(2,1)}, u32[]{:S(2)}) copy-start(bf16[384,3584]{1,0:T(8,128)(2,1)} %param.17) | copy-start | bytes 8257540
  19.1 37.8 %all-to-all-start = ((bf16[4,2,81920]{2,1,0:T(2,128)(2,1)}), bf16[4,2,81920]{2,1,0:T(2,128)(2,1)}, u32[]{:S(2)}, u32[]{:S(2)}) async-start(bf16[4,2,81920]{2,1,0:T(2,128)(2,1)} %reshape.322), calls=%async_computation | async-start | bytes 2621440 | tf_op jit(solution)/shard_map/all_to_all | solution.py:40
  56.9 86.3 %all-to-all-start.1 = ((bf16[4,2,229376]{2,1,0:T(2,128)(2,1)}), bf16[4,2,229376]{2,1,0:T(2,128)(2,1)}, u32[]{:S(2)}, u32[]{:S(2)}) async-start(bf16[4,2,229376]{2,1,0:T(2,128)(2,1)} %reshape.320), calls=%async_computation.1 | async-start | bytes 7340032 | tf_op jit(solution)/shard_map/all_to_all | solution.py:41
  61.8 184.0 %all-reduce.5.cloned.1.call-start = ((), (), s32[]{:S(2)}) async-start(), calls=%async_computation.10 | async-start | bytes 3145728 | tf_op jit(solution)/shard_map/psum | solution.py:47
  75.3 1.1 copy-start.3
  173.1 1.8 copy-start.2
  177.4 0.7 copy-start.8
  177.4 1.4 copy-start.7
  177.4 2.1 copy-start.10
  177.4 2.2 copy-start.9
  177.5 176.5 %all-gather.5.cloned.1.call-start = ((), (), s32[]{:S(2)}) async-start(), calls=%async_computation.6 | async-start | bytes 41287680 | tf_op jit(solution)/shard_map/all_gather | solution.py:38
  178.0 198.0 %reduce-scatter.6.cloned.1.call-start = ((), (), s32[]{:S(2)}) async-start(), calls=%async_computation.8 | async-start | bytes 3932160 | tf_op jit(solution)/shard_map/reduce_scatter | solution.py:75
  245.7 4.1 copy-start.5
  249.7 126.4 %reduce-scatter.8.cloned.1.call-start = ((), (), s32[]{:S(2)}) async-start(), calls=%async_computation.9 | async-start | bytes 11010048 | tf_op jit(solution)/shard_map/reduce_scatter | solution.py:76
  256.9 259.6 %all-gather.3.cloned.1.call-start = ((), (), s32[]{:S(2)}) async-start(), calls=%async_computation.5 | async-start | bytes 4915200 | tf_op jit(solution)/shard_map/all_gather | solution.py:37
  257.5 300.2 %reduce-scatter.4.cloned.1.call-start = ((), (), s32[]{:S(2)}) async-start(), calls=%async_computation.7 | async-start | bytes 9830400 | tf_op jit(solution)/shard_map/reduce_scatter | solution.py:62
  376.0 302.8 %all-reduce.7.cloned.1.call-start = ((), (), s32[]{:S(2)}) async-start(), calls=%async_computation.11 | async-start | bytes 9961472 | tf_op jit(solution)/shard_map/psum | solution.py:78
  540.0 17.8 %copy-start.4 = (bf16[4,2,64,1280]{3,2,1,0:T(8,128)(2,1)S(1)}, bf16[4,2,64,1280]{3,2,1,0:T(8,128)(2,1)}, u32[]{:S(2)}) copy-start(bf16[4,2,64,1280]{3,2,1,0:T(8,128)(2,1)} %copy-done.3) | copy-start | bytes 3932164
  540.0 17.8 %copy-start.6 = (f32[384,512]{1,0:T(8,128)S(1)}, f32[384,512]{1,0:T(8,128)}, u32[]{:S(2)}) copy-start(f32[384,512]{1,0:T(8,128)} %get-tuple-element.29) | copy-start | bytes 2359300
  678.8 6.8 copy-start.1
Sparse Core Ops, SparseCore 0:
  177.6 68.0 all-reduce.4
  249.9 16.8 reduce-scatter.5
  269.1 17.2 reduce-scatter.7
  376.1 181.5 reduce-scatter.3
  561.2 117.5 all-reduce.6
Sparse Core Ops, SparseCore 1:
  179.9 174.0 all-gather.4
  355.4 161.1 all-gather.2
where the time goes:
time: 695 us; the launch traced here: 693 us
  waiting for transfers between devices  494 us (71%)
  local copies, waits for them, and re-layouts  89.8 us (13%)
  matrix products  72.2 us (10%)
  between operations  15.4 us (2%)
  starting transfers between devices  11.6 us (2%)
  other arithmetic  9.35 us (1%)
    all_gather x1, waiting for transfers between devices, shards(): whole = lax.all_gather(tokens, 'tenant', axis=1, tiled=True)  140 us
    psum x1, waiting for transfers between devices, shards(): grad_down, grad_up = lax.psum((down_share, up_share), 'fsdp')  118 us
    all_gather x1, waiting for transfers between devices, shards(): lax.all_gather(frozen_up_weight, ('fsdp', 'dp'), axis=0, tiled=True)  96.2 us
    all_to_all x1, waiting for transfers between devices, shards(): lax.all_to_all(tenant_up_adapters, 'tenant', split_axis=2, concat_axis=0,...  64.2 us
    unnamed x30, local copies, waits for them, and re-layouts  58.2 us
    psum x1, waiting for transfers between devices, shards(): proj = lax.psum(partial_proj, 'tenant')  56.8 us
    dot_general x1, matrix products, shards(): base = jnp.dot(whole, weight, preferred_element_type=jnp.float32)  23.5 us
    dot_general x1, matrix products, shards(): lax.dot_general(cotangent, weight, (((1,), (1,)), ((), ())), preferred_el...  22.1 us
  transfers between devices with their start and end apart: 9, of which 7 were waited for; matrix products, arithmetic and copies ran while one was open for 17% of the time, Pallas kernels for 0%

commit v1 on v0

--- a/solution.py
+++ b/solution.py
@@ -34,7 +34,7 @@
     tenants = ranks.shape[0]
     largest_rank = tenant_down_adapters.shape[1]
     gain = make_gain(block_tenant_index, ranks, rows, largest_rank)
-    whole = lax.all_gather(tokens, "tenant", axis=1, tiled=True)
+    whole = jnp.concatenate(lax.all_gather(tokens, "tenant"), axis=1)
     weight = lax.all_gather(frozen_up_weight, ("fsdp", "dp"), axis=0, tiled=True)
     down_part, up_adapter_slice = (
         lax.all_to_all(tenant_down_adapters, "tenant", split_axis=2, concat_axis=0, tiled=True),

time: 695 us -> 695 us (level)
  transfers between devices with their start and end apart: 9 -> 9, of which waited for: 7 -> 7; matrix products, arithmetic and copies ran while one was open for 17% -> 18% of each run, Pallas kernels for 0% -> 0%
where the time goes in v1:
time: 695 us; the launch traced here: 693 us
  waiting for transfers between devices  488 us (70%)
  local copies, waits for them, and re-layouts  96.1 us (14%)
  matrix products  72.6 us (10%)
  between operations  15.4 us (2%)
  starting transfers between devices  11.6 us (2%)
  other arithmetic  9.35 us (1%)
    all_gather x1, waiting for transfers between devices, shards(): whole = jnp.concatenate(lax.all_gather(tokens, 'tenant'), axis=1)  140 us
    psum x1, waiting for transfers between devices, shards(): grad_down, grad_up = lax.psum((down_share, up_share), 'fsdp')  118 us
    all_gather x1, waiting for transfers between devices, shards(): lax.all_gather(frozen_up_weight, ('fsdp', 'dp'), axis=0, tiled=True)  96.2 us
    all_to_all x1, waiting for transfers between devices, shards(): lax.all_to_all(tenant_up_adapters, 'tenant', split_axis=2, concat_axis=0,...  64.2 us
    unnamed x30, local copies, waits for them, and re-layouts  58.2 us
    psum x1, waiting for transfers between devices, shards(): proj = lax.psum(partial_proj, 'tenant')  56.8 us
    dot_general x1, matrix products, shards(): base = jnp.dot(whole, weight, preferred_element_type=jnp.float32)  23.8 us
    dot_general x1, matrix products, shards(): lax.dot_general(cotangent, weight, (((1,), (1,)), ((), ())), preferred_el...  22.1 us
  transfers between devices with their start and end apart: 9, of which 7 were waited for; matrix products, arithmetic and copies ran while one was open for 18% of the time, Pallas kernels for 0%

profile of v1, /device:TPU:0, one launch (start us, length us, event | category | flops | bytes accessed | tf_op | source)
XLA Modules:
  0.0 692.7 jit_solution(10970325565534262289)
XLA Ops:
  8.0 0.0 copy-start
  8.0 6.4 copy.15
  14.5 4.7 reshape.331
  19.1 6.3 all-to-all-start
  25.5 15.8 %copy.18 = bf16[2,64,14336]{1,0,2:T(2,128)(2,1)} copy(bf16[2,64,14336]{2,1,0:T(8,128)(2,1)} %param.16) | data formatting | bytes 7340032 | tf_op args[5]
  41.3 8.6 %reshape.329 = bf16[4,2,229376]{2,1,0:T(2,128)(2,1)} reshape(bf16[14336,2,64]{2,1,0:T(2,128)(2,1)} %bitcast.81) | data formatting | bytes 7340032
  49.9 7.1 %all-to-all-done = bf16[4,2,81920]{2,1,0:T(2,128)(2,1)} async-done(((bf16[4,2,81920]{2,1,0:T(2,128)(2,1)}), bf16[4,2,81920]{2,1,0:T(2,128)(2,1)}, u32[]{:S(2)}, u32[]{:S(2)}) %all-to-all-start) | async-done | bytes 1310752 | tf_op jit(solution)/shard_map/all_to_all | solution.py:40
  56.9 4.8 all-to-all-start.1
  61.8 0.0 all-reduce.5.cloned.1.call-start
  61.8 4.6 reshape.332
  66.4 7.4 %copy.21 = bf16[2,64,4,1280]{3,2,1,0:T(4,128)(2,1)} copy(bf16[2,64,4,1280]{1,0,3,2:T(2,128)(2,1)} %bitcast.86) | data formatting | bytes 2621440 | tf_op jit(solution)/shard_map/all_to_all | solution.py:40
  73.8 1.4 copy.17
  75.3 0.0 copy-start.3
  75.3 1.0 copy-done.3
  76.3 2.8 fusion.26
  79.1 64.2 %all-to-all-done.1 = bf16[4,2,229376]{2,1,0:T(2,128)(2,1)} async-done(((bf16[4,2,229376]{2,1,0:T(2,128)(2,1)}), bf16[4,2,229376]{2,1,0:T(2,128)(2,1)}, u32[]{:S(2)}, u32[]{:S(2)}) %all-to-all-start.1) | async-done | bytes 3670048 | tf_op jit(solution)/shard_map/all_to_all | solution.py:41
  143.3 8.4 %reshape.330 = bf16[14336,2,64]{2,1,0:T(2,128)(2,1)} reshape(bf16[4,2,229376]{2,1,0:T(2,128)(2,1)} %all-to-all-done.1) | data formatting | bytes 7340032
  151.7 18.7 %copy.22 = bf16[2,64,4,3584]{3,2,1,0:T(4,128)(2,1)} copy(bf16[2,64,4,3584]{1,0,3,2:T(2,128)(2,1)} %bitcast.80) | data formatting | bytes 7340032 | tf_op jit(solution)/shard_map/all_to_all | solution.py:41
  170.4 2.7 copy.20
  173.1 0.0 copy-start.2
  173.1 1.8 copy-done.2
  174.9 0.0 copy-done
  174.9 2.5 fusion.28
  177.4 0.0 all-reduce.5.cloned.1.call-update
  177.5 0.0 all-gather.4.cloned.1.call-start
  177.5 0.5 all-gather.4.cloned.1.call-update
  178.0 0.0 reduce-scatter.6.cloned.1.call-start
  178.1 0.0 copy-done.8
  178.1 0.7 fusion.23
  178.8 0.0 copy-done.7
  178.8 0.7 fusion.24
  179.5 0.0 copy-done.10
  179.5 0.1 add_add_fusion.1
  179.6 0.0 copy-done.9
  179.6 0.1 fusion.8
  179.7 3.8 fusion.16
  183.5 4.5 compare_select_fusion.2
  188.0 0.8 fusion.12
  188.8 0.1 and_select_fusion
  188.9 56.8 %all-reduce.5.cloned.1.call-done = (f32[384,512]{1,0:T(8,128)}, f32[384,512]{1,0:T(8,128)}) async-done(((f32[384,512]{1,0:T(8,128)}, f32[384,512]{1,0:T(8,128)}), (f32[384,512]{1,0:T(8,128)}, f32[384,512]{1,0:T(8,128)})) %all-reduce.5.cloned.1.call-update) | async-done | bytes 1572880 | tf_op jit(solution)/shard_map/psum | solution.py:47
  245.7 4.0 fusion.17
  249.7 0.0 reduce-scatter.6.cloned.1.call-update
  249.7 0.0 reduce-scatter.8.cloned.1.call-start
  249.8 7.1 %fusion.20 = f32[512,3584]{1,0:T(8,128)} fusion(bf16[384,3584]{1,0:T(8,128)(2,1)S(1)} %copy-done, f32[384,512]{1,0:T(8,128)S(1)} %copy-done.5, f32[512]{0:T(512)S(1)} %convert_divide_fusion, s32[512]{0:T(512)S(1)} %add_select_fusion, s32[384]{0:T(512)S(1)} %and_select_fusion, pred[512]{0:T(512)(128)(4,1)S(1)} %get-tuple-element.32), kind=kOutput, calls=%fused_computation.52 | convolution fusion | flops 1410269184 | bytes 10885120 | tf_op jit(solution)/shard_map/dot_general | solution.py:66
  256.9 0.0 reduce-scatter.8.cloned.1.call-update
  256.9 0.0 all-gather.6.cloned.1.call-start
  256.9 0.5 all-gather.6.cloned.1.call-update
  257.5 0.2 reduce-scatter.4.cloned.1.call-start
  257.7 96.2 %all-gather.4.cloned.1.call-done = bf16[5120,3584]{1,0:T(8,128)(2,1)} async-done(((bf16[640,3584]{1,0:T(8,128)(2,1)}), bf16[5120,3584]{1,0:T(8,128)(2,1)}) %all-gather.4.cloned.1.call-update) | async-done | bytes 36700176 | tf_op jit(solution)/shard_map/all_gather | solution.py:38
  353.9 22.1 %fusion.27 = f32[384,5120]{1,0:T(8,128)} fusion(bf16[384,3584]{1,0:T(8,128)(2,1)S(1)} %copy-done, bf16[5120,3584]{1,0:T(8,128)(2,1)} %all-gather.4.cloned.1.call-done), kind=kOutput, calls=%fused_computation.57 | convolution fusion | flops 14092861440 | bytes 47316992 | tf_op jit(solution)/shard_map/dot_general | solution.py:59
  376.0 0.0 reduce-scatter.4.cloned.1.call-update
  376.0 0.0 all-reduce.7.cloned.1.call-start
  376.1 0.0 reduce-scatter.6.cloned.1.call-done
  376.1 0.0 reduce-scatter.8.cloned.1.call-done
  376.1 0.5 all-reduce.7.cloned.1.call-update
  376.6 139.9 %all-gather.6.cloned.1.call-done = bf16[1536,1280]{1,0:T(8,128)(2,1)} async-done(((bf16[384,1280]{1,0:T(8,128)(2,1)}), bf16[1536,1280]{1,0:T(8,128)(2,1)}) %all-gather.6.cloned.1.call-update) | async-done | bytes 3932176 | tf_op jit(solution)/shard_map/all_gather | solution.py:37
  516.5 6.3 copy.14
  522.8 23.8 %fusion.25 = f32[384,3584]{1,0:T(8,128)} fusion(bf16[384,5120]{0,1:T(8,128)(2,1)} %bitcast.92, bf16[5120,3584]{1,0:T(8,128)(2,1)} %all-gather.4.cloned.1.call-done), kind=kOutput, calls=%fused_computation.55 | convolution fusion | flops 14092861440 | bytes 46137344 | tf_op jit(solution)/shard_map/dot_general | solution.py:50
  546.6 7.1 %fusion = bf16[384,3584]{1,0:T(8,128)(2,1)} fusion(f32[384,3584]{1,0:T(8,128)} %fusion.25, bf16[512,3584]{1,0:T(8,128)(2,1)} %bitcast.83, f32[384,512]{1,0:T(8,128)S(1)} %copy-done.5, f32[512]{0:T(512)S(1)} %convert_divide_fusion, s32[512]{0:T(512)S(1)} %add_select_fusion, s32[384]{0:T(512)S(1)} %and_select_fusion, pred[512]{0:T(512)(128)(4,1)S(1)} %get-tuple-element.32), kind=kOutput, calls=%fused_computation.1 | convolution fusion | flops 1413021696 | bytes 12720128 | tf_op jit(solution)/shard_map/dot_general | solution.py:51
  553.7 4.0 reduce-scatter.4.cloned.1.call-done
  557.7 3.3 fusion.1
  561.0 117.8 %all-reduce.7.cloned.1.call-done = (f32[4,64,1280]{2,1,0:T(8,128)}, f32[4,64,3584]{2,1,0:T(8,128)}) async-done(((f32[4,64,1280]{2,1,0:T(8,128)}, f32[4,64,3584]{2,1,0:T(8,128)}), (f32[4,64,1280]{2,1,0:T(8,128)}, f32[4,64,3584]{2,1,0:T(8,128)})) %all-reduce.7.cloned.1.call-update) | async-done | bytes 4980752 | tf_op jit(solution)/shard_map/psum | solution.py:78
  678.8 2.6 copy.31
  681.4 4.1 copy.32
  (17 shorter events, 0.1 us)
Async XLA Ops:
  8.0 166.9 %copy-start = (bf16[384,3584]{1,0:T(8,128)(2,1)S(1)}, bf16[384,3584]{1,0:T(8,128)(2,1)}, u32[]{:S(2)}) copy-start(bf16[384,3584]{1,0:T(8,128)(2,1)} %param.17) | copy-start | bytes 8257540
  19.1 37.8 %all-to-all-start = ((bf16[4,2,81920]{2,1,0:T(2,128)(2,1)}), bf16[4,2,81920]{2,1,0:T(2,128)(2,1)}, u32[]{:S(2)}, u32[]{:S(2)}) async-start(bf16[4,2,81920]{2,1,0:T(2,128)(2,1)} %reshape.331), calls=%async_computation | async-start | bytes 2621440 | tf_op jit(solution)/shard_map/all_to_all | solution.py:40
  56.9 86.3 %all-to-all-start.1 = ((bf16[4,2,229376]{2,1,0:T(2,128)(2,1)}), bf16[4,2,229376]{2,1,0:T(2,128)(2,1)}, u32[]{:S(2)}, u32[]{:S(2)}) async-start(bf16[4,2,229376]{2,1,0:T(2,128)(2,1)} %reshape.329), calls=%async_computation.1 | async-start | bytes 7340032 | tf_op jit(solution)/shard_map/all_to_all | solution.py:41
  61.8 184.0 %all-reduce.5.cloned.1.call-start = ((), (), s32[]{:S(2)}) async-start(), calls=%async_computation.10 | async-start | bytes 3145728 | tf_op jit(solution)/shard_map/psum | solution.py:47
  75.3 1.1 copy-start.3
  173.1 1.8 copy-start.2
  177.4 0.7 copy-start.8
  177.4 1.4 copy-start.7
  177.4 2.1 copy-start.10
  177.4 2.2 copy-start.9
  177.5 176.5 %all-gather.4.cloned.1.call-start = ((), (), s32[]{:S(2)}) async-start(), calls=%async_computation.5 | async-start | bytes 41287680 | tf_op jit(solution)/shard_map/all_gather | solution.py:38
  178.0 198.0 %reduce-scatter.6.cloned.1.call-start = ((), (), s32[]{:S(2)}) async-start(), calls=%async_computation.7 | async-start | bytes 3932160 | tf_op jit(solution)/shard_map/reduce_scatter | solution.py:75
  245.7 4.1 copy-start.5
  249.7 126.4 %reduce-scatter.8.cloned.1.call-start = ((), (), s32[]{:S(2)}) async-start(), calls=%async_computation.8 | async-start | bytes 11010048 | tf_op jit(solution)/shard_map/reduce_scatter | solution.py:76
  256.9 259.6 %all-gather.6.cloned.1.call-start = ((), (), s32[]{:S(2)}) async-start(), calls=%async_computation.9 | async-start | bytes 4915200 | tf_op jit(solution)/shard_map/all_gather | solution.py:37
  257.5 300.2 %reduce-scatter.4.cloned.1.call-start = ((), (), s32[]{:S(2)}) async-start(), calls=%async_computation.6 | async-start | bytes 9830400 | tf_op jit(solution)/shard_map/reduce_scatter | solution.py:62
  376.0 302.8 %all-reduce.7.cloned.1.call-start = ((), (), s32[]{:S(2)}) async-start(), calls=%async_computation.11 | async-start | bytes 9961472 | tf_op jit(solution)/shard_map/psum | solution.py:78
  546.6 11.1 %copy-start.4 = (bf16[4,2,64,1280]{3,2,1,0:T(8,128)(2,1)S(1)}, bf16[4,2,64,1280]{3,2,1,0:T(8,128)(2,1)}, u32[]{:S(2)}) copy-start(bf16[4,2,64,1280]{3,2,1,0:T(8,128)(2,1)} %copy-done.3) | copy-start | bytes 3932164
  546.6 11.1 %copy-start.6 = (f32[384,512]{1,0:T(8,128)S(1)}, f32[384,512]{1,0:T(8,128)}, u32[]{:S(2)}) copy-start(f32[384,512]{1,0:T(8,128)} %get-tuple-element.29) | copy-start | bytes 2359300
  678.8 6.8 copy-start.1
Sparse Core Ops, SparseCore 0:
  177.6 68.0 all-reduce.4
  249.9 16.8 reduce-scatter.5
  269.1 17.2 reduce-scatter.7
  376.1 181.5 reduce-scatter.3
  561.2 117.5 all-reduce.6
Sparse Core Ops, SparseCore 1:
  179.9 174.0 all-gather.3
  355.4 161.1 all-gather.5
